TPU v7x, 32 devices: a whole 2x2x4 slice. The times are simulated.
32 devices in a mesh: img: 8 (over y, x, core), row: 4 (over z).
Axes of the slice: x: 2, y: 2, z: 4, core: 2. Of those that a mesh axis runs over, the one named last changes fastest.
Arguments:
- features: bfloat16 [8, 32, 384, 256], P('img', 'row'), may hold values from -6 to 6
- cotangent: bfloat16 [8, 32, 384, 256], P('img', 'row'), may hold values from -6 to 6
- weight_one: bfloat16 [3, 3, 256, 256], replicated, may hold values from -0.125 to 0.125
- weight_two: bfloat16 [3, 3, 256, 256], replicated, may hold values from -0.125 to 0.125
Outputs:
- input_grad: bfloat16 [8, 32, 384, 256], P('img', 'row')
- weight_one_grad: float32 [589824], P(('img', 'row'))
- weight_two_grad: float32 [589824], P(('img', 'row'))
All inputs are finite; a program needn't handle non-finite values.
Results may differ from a plain program's by a relative error of at most 0.0055.
Values may be sent and summed in bfloat16 or wider, within the bound.
No kernel may reach another device: no remote copies, remote signals or barrier semaphores. Data moves between devices by JAX's collectives and lax.ppermute only.
A program may use at most 128 MiB of HBM per device.

v0:
```python
import functools
import math

import jax
import jax.numpy as jnp
from jax import lax
from jax.experimental import pallas as pl
from jax.experimental.pallas import tpu as pltpu
from jax.sharding import PartitionSpec as P

COEFF = 0.7978845608028654
CUBE = 0.044715
F32 = jnp.float32
BF16 = jnp.bfloat16
VMEM = pl.BlockSpec(memory_space=pltpu.VMEM)
NT = (((1,), (1,)), ((), ()))


def gelu_parts(value):
    square = value * value
    tanhed = jnp.tanh(value * (COEFF + (COEFF * CUBE) * square))
    half = 0.5 + 0.5 * tanhed
    return (square, half, value * half)


def gelu_slope(square, half, gated):
    return half + gated * (1.0 - half) * (2.0 * COEFF + (6.0 * COEFF * CUBE) * square)


def column_shifts(field):
    cols = field.shape[0]
    spot = lax.broadcasted_iota(jnp.int32, field.shape, 0)
    left = jnp.where(spot == 0, 0.0, pltpu.roll(field, 1, 0))
    right = jnp.where(spot == cols - 1, 0.0, pltpu.roll(field, cols - 1, 0))
    return (left.astype(BF16), field.astype(BF16), right.astype(BF16))


def hidden_kernel(rows, cols, chans, block, f_ref, c_ref, w1_ref, w2_ref, hg_ref, at_ref, g2_ref, x3, c3, gt):
    def prepare(r, carry):
        base = pl.multiple_of(r * cols, cols)
        _, _, acted = gelu_parts(f_ref[r].astype(F32))
        left, mid, right = column_shifts(acted)
        x3[pl.ds(base, cols), 0:chans] = left
        x3[pl.ds(base, cols), chans : 2 * chans] = mid
        x3[pl.ds(base, cols), 2 * chans : 3 * chans] = right
        at_ref[:, pl.ds(base, cols)] = mid.T
        left, mid, right = column_shifts(c_ref[r].astype(F32))
        c3[pl.ds(base, cols), 0:chans] = right
        c3[pl.ds(base, cols), chans : 2 * chans] = mid
        c3[pl.ds(base, cols), 2 * chans : 3 * chans] = left
        return carry

    lax.fori_loop(0, rows + 2, prepare, 0)
    size = block * cols

    def convolve(step, carry):
        hidden = jnp.zeros((size, chans), F32)
        back = jnp.zeros((size, chans), F32)
        for a in range(3):
            ahead = pl.multiple_of((step * block + a) * cols, cols)
            behind = pl.multiple_of((step * block + 2 - a) * cols, cols)
            for b in range(3):
                part = slice(b * chans, (b + 1) * chans)
                hidden += jnp.dot(x3[pl.ds(ahead, size), part], w1_ref[a, b], preferred_element_type=F32)
                back += lax.dot_general(c3[pl.ds(behind, size), part], w2_ref[a, b], NT, preferred_element_type=F32)
        square, half, gated = gelu_parts(hidden)
        base = pl.multiple_of(step * size, size)
        gt[:, pl.ds(base, size)] = gated.astype(BF16).T
        hg_ref[pl.ds(base, size), :] = (back * gelu_slope(square, half, gated)).astype(BF16)
        return carry

    lax.fori_loop(0, rows // block, convolve, 0)
    for a in range(3):
        for b in range(3):
            g2_ref[a, b] = jnp.dot(
                gt[...], c3[(2 - a) * cols : (2 - a + rows) * cols, b * chans : (b + 1) * chans],
                preferred_element_type=F32,
            ).astype(BF16)


def grad_kernel(rows, cols, chans, hg_ref, at_ref, g1_ref, h3_ref):
    def prepare(r, carry):
        base = pl.multiple_of(r * cols, cols)
        left, mid, right = column_shifts(hg_ref[pl.ds(base, cols), :].astype(F32))
        h3_ref[pl.ds(base, cols), 0:chans] = right
        h3_ref[pl.ds(base, cols), chans : 2 * chans] = mid
        h3_ref[pl.ds(base, cols), 2 * chans : 3 * chans] = left
        return carry

    lax.fori_loop(0, rows, prepare, 0)
    for a in range(3):
        for b in range(3):
            g1_ref[a, b] = jnp.dot(
                at_ref[:, a * cols : (a + rows) * cols], h3_ref[:, b * chans : (b + 1) * chans],
                preferred_element_type=F32,
            ).astype(BF16)


def input_kernel(rows, cols, chans, block, h3_ref, top_ref, low_ref, f_ref, c_ref, w1_ref, out_ref, h3):
    h3[cols : (rows + 1) * cols, :] = h3_ref[...]
    for ref, r in ((top_ref, 0), (low_ref, rows + 1)):
        left, mid, right = column_shifts(ref[...].astype(F32))
        h3[r * cols : (r + 1) * cols, 0:chans] = right
        h3[r * cols : (r + 1) * cols, chans : 2 * chans] = mid
        h3[r * cols : (r + 1) * cols, 2 * chans : 3 * chans] = left
    size = block * cols

    def convolve(step, carry):
        back = jnp.zeros((size, chans), F32)
        for a in range(3):
            behind = pl.multiple_of((step * block + 2 - a) * cols, cols)
            for b in range(3):
                part = slice(b * chans, (b + 1) * chans)
                back += lax.dot_general(h3[pl.ds(behind, size), part], w1_ref[a, b], NT, preferred_element_type=F32)
        here = pl.ds(pl.multiple_of(step * size, size), size)
        slope = gelu_slope(*gelu_parts(f_ref[here, :].astype(F32)))
        out_ref[here, :] = (c_ref[here, :].astype(F32) + back * slope).astype(BF16)
        return carry

    lax.fori_loop(0, rows // block, convolve, 0)


def exchange(flat, axis):
    peers = lax.axis_size(axis)
    parts = flat.reshape(peers, flat.shape[0] // peers, flat.shape[1])
    parts = lax.all_to_all(parts, axis, 0, 0)
    return jnp.sum(parts.astype(F32), axis=0)


def shards(features, cotangent, weight_one, weight_two):
    _, rows, cols, chans = features.shape
    peers = lax.axis_size("row")
    height = rows * peers
    down = [(i, i + 1) for i in range(peers - 1)]
    up = [(j, i) for i, j in down]
    both = jnp.stack([features[0], cotangent[0]])
    before = lax.ppermute(both[:, rows - 1 :], "row", down)
    after = lax.ppermute(both[:, :1], "row", up)
    wide = jnp.concatenate([before, both, after], axis=1)
    block = 4
    shape = jax.ShapeDtypeStruct
    cells = rows * cols
    hidden_grad, acted_t, grad_two = pl.pallas_call(
        functools.partial(hidden_kernel, rows, cols, chans, block),
        out_shape=(
            shape((cells, chans), BF16),
            shape((chans, cells + 2 * cols), BF16),
            shape((3, 3, chans, chans), BF16),
        ),
        in_specs=[VMEM] * 4,
        out_specs=[VMEM] * 3,
        scratch_shapes=[
            pltpu.VMEM((cells + 2 * cols, 3 * chans), BF16),
            pltpu.VMEM((cells + 2 * cols, 3 * chans), BF16),
            pltpu.VMEM((chans, cells), BF16),
        ],
        name="hidden",
    )(wide[0], wide[1], weight_one, weight_two)
    top = lax.ppermute(hidden_grad[cells - cols :], "row", down)
    low = lax.ppermute(hidden_grad[:cols], "row", up)
    grad_one, hidden_shifts = pl.pallas_call(
        functools.partial(grad_kernel, rows, cols, chans),
        out_shape=(shape((3, 3, chans, chans), BF16), shape((cells, 3 * chans), BF16)),
        in_specs=[VMEM] * 2,
        out_specs=[VMEM] * 2,
        name="grad",
    )(hidden_grad, acted_t)
    input_grad = pl.pallas_call(
        functools.partial(input_kernel, rows, cols, chans, block),
        out_shape=shape((cells, chans), BF16),
        in_specs=[VMEM] * 6,
        out_specs=VMEM,
        scratch_shapes=[pltpu.VMEM((cells + 2 * cols, 3 * chans), BF16)],
        name="input",
    )(hidden_shifts, top, low, features.reshape(cells, chans), cotangent.reshape(cells, chans), weight_one)
    scale = 1.0 / math.sqrt(lax.axis_size("img") * height * cols)
    outs = []
    for grad in (grad_one, grad_two):
        part = exchange(grad.reshape(9 * chans, chans), "img").astype(BF16)
        outs.append((exchange(part, "row") * scale).reshape(-1))
    return (input_grad.reshape(features.shape), outs[0], outs[1])


def solution(mesh):
    placed = (P("img", "row", None, None), P("img", "row", None, None), P(), P())
    return jax.shard_map(
        shards,
        mesh=mesh,
        in_specs=placed,
        out_specs=(P("img", "row", None, None), P(("img", "row")), P(("img", "row"))),
        check_vma=False,
    )
```

profile of v0, /device:TPU:0, one launch (start us, length us, event | category | flops | bytes accessed | tf_op | source)
XLA Modules:
  0.0 123.1 jit_solution(10683321079190506250)
XLA Ops:
  0.6 0.0 copy-start
  0.6 1.6 %constant_dynamic-update-slice_fusion.1 = bf16[2,8,384,256]{3,2,1,0:T(8,128)(2,1)S(1)} fusion(bf16[1,8,384,256]{3,2,1,0:T(8,128)(2,1)} %param.4), kind=kLoop, calls=%fused_computation.8 | loop fusion | bytes 3145728
  2.3 0.2 copy-done
  2.5 0.1 constant_dynamic-update-slice_fusion
  2.6 0.1 fusion
  2.7 5.0 %collective-permute-start = (bf16[2,1,384,256]{3,2,1,0:T(8,128)(2,1)S(1)}, bf16[2,1,384,256]{3,2,1,0:T(8,128)(2,1)S(1)}, u32[]{:S(2)}, u32[]{:S(2)}) collective-permute-start(bf16[2,1,384,256]{3,2,1,0:T(8,128)(2,1)S(1)} %get-tuple-element.15), channel_id=1, source_target_pairs={{0,1},{1,2},{2,3},{4,5},{5,6},{6,7},{8,9},{9,10},{10,11},{12,13},{... | collective-permute-start | bytes 1179656 | tf_op jit(solution)/shard_map/ppermute | solution.py:137
  7.7 1.3 %collective-permute-start.1 = (bf16[2,1,384,256]{3,2,1,0:T(8,128)(2,1)S(1)}, bf16[2,1,384,256]{3,2,1,0:T(8,128)(2,1)S(1)}, u32[]{:S(2)}, u32[]{:S(2)}) collective-permute-start(bf16[2,1,384,256]{3,2,1,0:T(8,128)(2,1)S(1)} %get-tuple-element.16), channel_id=1, source_target_pairs={{1,0},{2,1},{3,2},{5,4},{6,5},{7,6},{9,8},{10,9},{11,10},{13,12},{... | collective-permute-start | bytes 1179656 | tf_op jit(solution)/shard_map/ppermute | solution.py:138
  9.0 7.0 %collective-permute-done = bf16[2,1,384,256]{3,2,1,0:T(8,128)(2,1)S(1)} collective-permute-done((bf16[2,1,384,256]{3,2,1,0:T(8,128)(2,1)S(1)}, bf16[2,1,384,256]{3,2,1,0:T(8,128)(2,1)S(1)}, u32[]{:S(2)}, u32[]{:S(2)}) %collective-permute-start) | collective-permute-done | bytes 393248 | tf_op jit(solution)/shard_map/ppermute | solution.py:137
  16.0 4.1 %collective-permute-done.1 = bf16[2,1,384,256]{3,2,1,0:T(8,128)(2,1)S(1)} collective-permute-done((bf16[2,1,384,256]{3,2,1,0:T(8,128)(2,1)S(1)}, bf16[2,1,384,256]{3,2,1,0:T(8,128)(2,1)S(1)}, u32[]{:S(2)}, u32[]{:S(2)}) %collective-permute-start.1) | collective-permute-done | bytes 393248 | tf_op jit(solution)/shard_map/ppermute | solution.py:138
  20.1 0.5 pad_maximum_fusion
  20.7 2.1 %slice_bitcast_fusion = (bf16[10,384,256]{2,1,0:T(8,128)(2,1)}, bf16[10,384,256]{2,1,0:T(8,128)(2,1)}) fusion(bf16[2,10,384,256]{3,2,1,0:T(8,128)(2,1)S(1)} %pad_maximum_fusion), kind=kLoop, calls=%fused_computation.1 | loop fusion | bytes 7864320 | tf_op jit(solution)/shard_map/squeeze | solution.py:158
  22.8 20.7 %hidden.1 = (bf16[3072,256]{1,0:T(8,128)(2,1)}, bf16[256,3840]{1,0:T(8,128)(2,1)}, bf16[3,3,256,256]{3,2,1,0:T(8,128)(2,1)}) custom-call(bf16[10,384,256]{2,1,0:T(8,128)(2,1)} %get-tuple-element.14.f_ref, bf16[10,384,256]{2,1,0:T(8,128)(2,1)} %get-tuple-element.13.c_ref, bf16[3,3,256,256]{3,2,1,0:T(8,128)(2,1)} %w1_ref.3, bf16[3,3,256,256]{3,2,1,0:T(8,128)(2,1)} %w2_ref.1), custom_call_target="tpu_custom_call" | custom-call | tf_op jit(solution)/shard_map/hidden/pallas_call | solution.py:143
  43.5 3.7 %all-to-all-start.2 = ((bf16[8,288,256]{2,1,0:T(8,128)(2,1)}), bf16[8,288,256]{2,1,0:T(8,128)(2,1)S(1)}, u32[]{:S(2)}, u32[]{:S(2)}) async-start(bf16[8,288,256]{2,1,0:T(8,128)(2,1)} %bitcast.21), calls=%async_computation.2 | async-start | bytes 2359296 | tf_op jit(solution)/shard_map/all_to_all | solution.py:126
  47.2 7.8 %grad.1 = (bf16[3,3,256,256]{3,2,1,0:T(8,128)(2,1)}, bf16[3072,768]{1,0:T(8,128)(2,1)}) custom-call(bf16[3072,256]{1,0:T(8,128)(2,1)} %get-tuple-element.8.hg_ref, bf16[256,3840]{1,0:T(8,128)(2,1)} %get-tuple-element.9.at_ref), custom_call_target="tpu_custom_call" | custom-call | tf_op jit(solution)/shard_map/grad/pallas_call | solution.py:161
  54.9 9.0 %all-to-all-done.2 = bf16[8,288,256]{2,1,0:T(8,128)(2,1)S(1)} async-done(((bf16[8,288,256]{2,1,0:T(8,128)(2,1)}), bf16[8,288,256]{2,1,0:T(8,128)(2,1)S(1)}, u32[]{:S(2)}, u32[]{:S(2)}) %all-to-all-start.2) | async-done | bytes 1179680 | tf_op jit(solution)/shard_map/all_to_all | solution.py:126
  64.0 3.6 %all-to-all-start = ((bf16[8,288,256]{2,1,0:T(8,128)(2,1)}), bf16[8,288,256]{2,1,0:T(8,128)(2,1)S(1)}, u32[]{:S(2)}, u32[]{:S(2)}) async-start(bf16[8,288,256]{2,1,0:T(8,128)(2,1)} %bitcast.20), calls=%async_computation | async-start | bytes 2359296 | tf_op jit(solution)/shard_map/all_to_all | solution.py:126
  67.5 0.8 reduce_sum.44
  68.4 15.9 %all-to-all-done = bf16[8,288,256]{2,1,0:T(8,128)(2,1)S(1)} async-done(((bf16[8,288,256]{2,1,0:T(8,128)(2,1)}), bf16[8,288,256]{2,1,0:T(8,128)(2,1)S(1)}, u32[]{:S(2)}, u32[]{:S(2)}) %all-to-all-start) | async-done | bytes 1179680 | tf_op jit(solution)/shard_map/all_to_all | solution.py:126
  84.2 3.8 %all-to-all-start.3 = ((bf16[4,72,256]{2,1,0:T(8,128)(2,1)}), bf16[4,72,256]{2,1,0:T(8,128)(2,1)S(1)}, u32[]{:S(2)}, u32[]{:S(2)}) async-start(bf16[4,72,256]{2,1,0:T(8,128)(2,1)} %bitcast.8), calls=%async_computation.3 | async-start | bytes 294912 | tf_op jit(solution)/shard_map/all_to_all | solution.py:126
  88.1 1.0 fusion.1
  89.1 1.3 %collective-permute-start.3 = (bf16[384,256]{1,0:T(8,128)(2,1)S(1)}, bf16[384,256]{1,0:T(8,128)(2,1)S(1)}, u32[]{:S(2)}, u32[]{:S(2)}) collective-permute-start(bf16[384,256]{1,0:T(8,128)(2,1)S(1)} %get-tuple-element.17), channel_id=1, source_target_pairs={{1,0},{2,1},{3,2},{5,4},{6,5},{7,6},{9,8},{10,9},{11,10},{13,12},{... | collective-permute-start | bytes 589832 | tf_op jit(solution)/shard_map/ppermute | solution.py:160
  90.4 4.6 %collective-permute-start.2 = (bf16[384,256]{1,0:T(8,128)(2,1)S(1)}, bf16[384,256]{1,0:T(8,128)(2,1)S(1)}, u32[]{:S(2)}, u32[]{:S(2)}) collective-permute-start(bf16[384,256]{1,0:T(8,128)(2,1)S(1)} %get-tuple-element.18), channel_id=1, source_target_pairs={{0,1},{1,2},{2,3},{4,5},{5,6},{6,7},{8,9},{9,10},{10,11},{12,13},{... | collective-permute-start | bytes 589832 | tf_op jit(solution)/shard_map/ppermute | solution.py:159
  95.0 1.8 %collective-permute-done.3.low_ref = bf16[384,256]{1,0:T(8,128)(2,1)S(1)} collective-permute-done((bf16[384,256]{1,0:T(8,128)(2,1)S(1)}, bf16[384,256]{1,0:T(8,128)(2,1)S(1)}, u32[]{:S(2)}, u32[]{:S(2)}) %collective-permute-start.3) | collective-permute-done | bytes 196640 | tf_op jit(solution)/shard_map/ppermute | solution.py:160
  96.8 1.4 %collective-permute-done.2.top_ref = bf16[384,256]{1,0:T(8,128)(2,1)S(1)} collective-permute-done((bf16[384,256]{1,0:T(8,128)(2,1)S(1)}, bf16[384,256]{1,0:T(8,128)(2,1)S(1)}, u32[]{:S(2)}, u32[]{:S(2)}) %collective-permute-start.2) | collective-permute-done | bytes 196640 | tf_op jit(solution)/shard_map/ppermute | solution.py:159
  98.2 0.7 copy-done.2
  98.9 10.7 %input.1 = bf16[3072,256]{1,0:T(8,128)(2,1)} custom-call(bf16[3072,768]{1,0:T(8,128)(2,1)} %get-tuple-element.10.h3_ref, bf16[384,256]{1,0:T(8,128)(2,1)} %copy-done.2, bf16[384,256]{1,0:T(8,128)(2,1)} %copy-done.1, bf16[3072,256]{1,0:T(8,128)(2,1)} %bitcast.17, bf16[3072,256]{1,0:T(8,128)(2,1)} %bitcast.18, bf16[3,3,256,256]{3,2,1,0:T(8,128)(2,1)} %w1_ref.3), custom_call_target="tpu_custom_call" | custom-call | tf_op jit(solution)/shard_map/input/pallas_call | solution.py:168
  109.5 0.8 reduce_sum.42
  110.4 0.0 all-to-all-done.3
  110.4 6.1 %all-to-all-start.1 = ((bf16[4,72,256]{2,1,0:T(8,128)(2,1)}), bf16[4,72,256]{2,1,0:T(8,128)(2,1)S(1)}, u32[]{:S(2)}, u32[]{:S(2)}) async-start(bf16[4,72,256]{2,1,0:T(8,128)(2,1)} %bitcast.6), calls=%async_computation.1 | async-start | bytes 294912 | tf_op jit(solution)/shard_map/all_to_all | solution.py:126
  116.5 0.7 copy.8
  117.2 5.3 %all-to-all-done.1 = bf16[4,72,256]{2,1,0:T(8,128)(2,1)S(1)} async-done(((bf16[4,72,256]{2,1,0:T(8,128)(2,1)}), bf16[4,72,256]{2,1,0:T(8,128)(2,1)S(1)}, u32[]{:S(2)}, u32[]{:S(2)}) %all-to-all-start.1) | async-done | bytes 147488 | tf_op jit(solution)/shard_map/all_to_all | solution.py:126
  122.5 0.7 copy.7
  (7 shorter events, 0.1 us)
Async XLA Ops:
  0.6 1.9 %copy-start = (bf16[1,8,384,256]{3,2,1,0:T(8,128)(2,1)S(1)}, bf16[1,8,384,256]{3,2,1,0:T(8,128)(2,1)}, u32[]{:S(2)}) copy-start(bf16[1,8,384,256]{3,2,1,0:T(8,128)(2,1)} %param.5) | copy-start | bytes 4718596
  2.7 13.3 %collective-permute-start = (bf16[2,1,384,256]{3,2,1,0:T(8,128)(2,1)S(1)}, bf16[2,1,384,256]{3,2,1,0:T(8,128)(2,1)S(1)}, u32[]{:S(2)}, u32[]{:S(2)}) collective-permute-start(bf16[2,1,384,256]{3,2,1,0:T(8,128)(2,1)S(1)} %get-tuple-element.15), channel_id=1, source_target_pairs={{0,1},{1,2},{2,3},{4,5},{5,6},{6,7},{8,9},{9,10},{10,11},{12,13},{... | collective-permute-start | bytes 1179656 | tf_op jit(solution)/shard_map/ppermute | solution.py:137
  7.7 12.5 %collective-permute-start.1 = (bf16[2,1,384,256]{3,2,1,0:T(8,128)(2,1)S(1)}, bf16[2,1,384,256]{3,2,1,0:T(8,128)(2,1)S(1)}, u32[]{:S(2)}, u32[]{:S(2)}) collective-permute-start(bf16[2,1,384,256]{3,2,1,0:T(8,128)(2,1)S(1)} %get-tuple-element.16), channel_id=1, source_target_pairs={{1,0},{2,1},{3,2},{5,4},{6,5},{7,6},{9,8},{10,9},{11,10},{13,12},{... | collective-permute-start | bytes 1179656 | tf_op jit(solution)/shard_map/ppermute | solution.py:138
  43.5 20.5 %all-to-all-start.2 = ((bf16[8,288,256]{2,1,0:T(8,128)(2,1)}), bf16[8,288,256]{2,1,0:T(8,128)(2,1)S(1)}, u32[]{:S(2)}, u32[]{:S(2)}) async-start(bf16[8,288,256]{2,1,0:T(8,128)(2,1)} %bitcast.21), calls=%async_computation.2 | async-start | bytes 2359296 | tf_op jit(solution)/shard_map/all_to_all | solution.py:126
  64.0 20.3 %all-to-all-start = ((bf16[8,288,256]{2,1,0:T(8,128)(2,1)}), bf16[8,288,256]{2,1,0:T(8,128)(2,1)S(1)}, u32[]{:S(2)}, u32[]{:S(2)}) async-start(bf16[8,288,256]{2,1,0:T(8,128)(2,1)} %bitcast.20), calls=%async_computation | async-start | bytes 2359296 | tf_op jit(solution)/shard_map/all_to_all | solution.py:126
  84.2 26.1 %all-to-all-start.3 = ((bf16[4,72,256]{2,1,0:T(8,128)(2,1)}), bf16[4,72,256]{2,1,0:T(8,128)(2,1)S(1)}, u32[]{:S(2)}, u32[]{:S(2)}) async-start(bf16[4,72,256]{2,1,0:T(8,128)(2,1)} %bitcast.8), calls=%async_computation.3 | async-start | bytes 294912 | tf_op jit(solution)/shard_map/all_to_all | solution.py:126
  89.1 7.6 %collective-permute-start.3 = (bf16[384,256]{1,0:T(8,128)(2,1)S(1)}, bf16[384,256]{1,0:T(8,128)(2,1)S(1)}, u32[]{:S(2)}, u32[]{:S(2)}) collective-permute-start(bf16[384,256]{1,0:T(8,128)(2,1)S(1)} %get-tuple-element.17), channel_id=1, source_target_pairs={{1,0},{2,1},{3,2},{5,4},{6,5},{7,6},{9,8},{10,9},{11,10},{13,12},{... | collective-permute-start | bytes 589832 | tf_op jit(solution)/shard_map/ppermute | solution.py:160
  90.4 7.7 %collective-permute-start.2 = (bf16[384,256]{1,0:T(8,128)(2,1)S(1)}, bf16[384,256]{1,0:T(8,128)(2,1)S(1)}, u32[]{:S(2)}, u32[]{:S(2)}) collective-permute-start(bf16[384,256]{1,0:T(8,128)(2,1)S(1)} %get-tuple-element.18), channel_id=1, source_target_pairs={{0,1},{1,2},{2,3},{4,5},{5,6},{6,7},{8,9},{9,10},{10,11},{12,13},{... | collective-permute-start | bytes 589832 | tf_op jit(solution)/shard_map/ppermute | solution.py:159
  96.8 1.4 %copy-start.1 = (bf16[384,256]{1,0:T(8,128)(2,1)}, bf16[384,256]{1,0:T(8,128)(2,1)S(1)}, u32[]{:S(2)}) copy-start(bf16[384,256]{1,0:T(8,128)(2,1)S(1)} %collective-permute-done.3.low_ref) | copy-start | bytes 589828
  98.2 0.7 copy-start.2
  110.4 12.1 %all-to-all-start.1 = ((bf16[4,72,256]{2,1,0:T(8,128)(2,1)}), bf16[4,72,256]{2,1,0:T(8,128)(2,1)S(1)}, u32[]{:S(2)}, u32[]{:S(2)}) async-start(bf16[4,72,256]{2,1,0:T(8,128)(2,1)} %bitcast.6), calls=%async_computation.1 | async-start | bytes 294912 | tf_op jit(solution)/shard_map/all_to_all | solution.py:126
where the time goes:
time: 124 us; the launch traced here: 123 us
  waiting for transfers between devices  44.5 us (36%)
  Pallas kernels  39.1 us (32%)
  starting transfers between devices  29.4 us (24%)
  local copies, waits for them, and re-layouts  7.23 us (6%)
  other arithmetic  2.24 us (2%)
    all_to_all x4, waiting for transfers between devices, exchange(): parts = lax.all_to_all(parts, axis, 0, 0)  30.2 us
    pallas_call x1, Pallas kernels, shards(): pl.pallas_call(functools.partial(hidden_kernel, rows, cols, chans, block)...  20.7 us
    all_to_all x4, starting transfers between devices, exchange(): parts = lax.all_to_all(parts, axis, 0, 0)  17.2 us
    pallas_call x1, Pallas kernels, shards(): pl.pallas_call(functools.partial(input_kernel, rows, cols, chans, block),...  10.7 us
    pallas_call x1, Pallas kernels, shards(): pl.pallas_call(functools.partial(grad_kernel, rows, cols, chans), out_sha...  7.75 us
    ppermute x1, waiting for transfers between devices, shards(): before = lax.ppermute(both[:, rows - 1:], 'row', down)  7.03 us
    ppermute x1, starting transfers between devices, shards(): before = lax.ppermute(both[:, rows - 1:], 'row', down)  4.98 us
    ppermute x1, starting transfers between devices, shards(): top = lax.ppermute(hidden_grad[cells - cols:], 'row', down)  4.57 us
  transfers between devices with their start and end apart: 8, of which 7 were waited for; matrix products, arithmetic and copies ran while one was open for 3% of the time, Pallas kernels for 15%

commit v1 on v0

v1 whole, which is shorter than its diff:
```python
import functools
import math

import jax
import jax.numpy as jnp
from jax import lax
from jax.experimental import pallas as pl
from jax.experimental.pallas import tpu as pltpu
from jax.sharding import PartitionSpec as P


COEFF = 0.7978845608028654
CUBE = 0.044715
F32 = jnp.float32
BF16 = jnp.bfloat16
VMEM = pl.BlockSpec(memory_space=pltpu.VMEM)
SMEM = pl.BlockSpec(memory_space=pltpu.SMEM)
NN = (((1,), (0,)), ((), ()))
NT = (((1,), (1,)), ((), ()))
MIB = 1024 * 1024


def gelu_parts(value):
    square = value * value
    tanhed = jnp.tanh(value * (COEFF + (COEFF * CUBE) * square))
    half = 0.5 + 0.5 * tanhed
    return (square, half, value * half)


def gelu_slope(square, half, gated):
    return half + gated * (1.0 - half) * (2.0 * COEFF + (6.0 * COEFF * CUBE) * square)


def column_shifts(field):
    cols = field.shape[0]
    spot = lax.broadcasted_iota(jnp.int32, field.shape, 0)
    left = jnp.where(spot == 0, 0.0, pltpu.roll(field, 1, 0))
    right = jnp.where(spot == cols - 1, 0.0, pltpu.roll(field, cols - 1, 0))
    return (left.astype(BF16), field.astype(BF16), right.astype(BF16))


def put_shifts(ref, base, cols, shifts):
    chans = shifts[0].shape[1]
    for b, value in enumerate(shifts):
        ref[pl.ds(base, cols), b * chans : (b + 1) * chans] = value


def dot(left, right, dims=NN):
    return lax.dot_general(left, right, dims, preferred_element_type=F32)


def conv(windows, weight, dims):
    chans = weight.shape[-1]
    total = None
    for a in range(3):
        for b in range(3):
            part = slice(b * chans, (b + 1) * chans)
            terms = [dot(ref[start : start + length, part], weight[a, b], dims) for ref, start, length in windows[a]]
            term = terms[0] if len(terms) == 1 else jnp.concatenate(terms, axis=0)
            total = term if total is None else total + term
    return total


def window(own, top, low, first, count, rows, cols):
    pieces = []
    if first < 0:
        pieces.append((top, 0, cols))
    begin, end = max(first, 0), min(first + count, rows)
    if end > begin:
        pieces.append((own, begin * cols, (end - begin) * cols))
    if first + count > rows:
        pieces.append((low, 0, cols))
    return pieces


def is_even():
    return lax.axis_index("row") % 2 == 0


def pack_kernel(f_first, f_last, c_first, c_last, to_a, to_b):
    even = is_even()
    for i, (head, tail) in enumerate(((f_first, f_last), (c_first, c_last))):
        to_a[i] = jnp.where(even, tail[...], head[...])
        to_b[i] = jnp.where(even, head[...], tail[...])


def inner_kernel(rows, cols, f_ref, c_ref, w1_ref, x3, c3, at, gt, slope):
    def prepare(r, carry):
        base = pl.multiple_of(r * cols, cols)
        acted = gelu_parts(f_ref[pl.ds(base, cols), :].astype(F32))[2]
        shifts = column_shifts(acted)
        put_shifts(x3, base, cols, shifts)
        at[:, pl.ds(base, cols)] = shifts[1].T
        put_shifts(c3, base, cols, column_shifts(c_ref[pl.ds(base, cols), :].astype(F32))[::-1])
        return carry

    lax.fori_loop(0, rows, prepare, 0)
    block = (rows - 2) // 2
    for first in (1, 1 + block):
        hidden = conv([window(x3, None, None, first - 1 + a, block, rows, cols) for a in range(3)], w1_ref, NN)
        parts = gelu_parts(hidden)
        here = slice((first - 1) * cols, (first - 1 + block) * cols)
        gt[:, here] = parts[2].astype(BF16).T
        slope[here, :] = gelu_slope(*parts)


def place(box, value, tap):
    core, chip, size = lax.axis_index("img") % 2, lax.axis_index("img") // 2, box.shape[2]
    start = tap * value.shape[0]
    row = start
    while row < start + value.shape[0]:
        index, offset = divmod(row, size)
        count = min(size - offset, start + value.shape[0] - row)
        box[(index % 2) ^ core, (index // 2) ^ chip, offset : offset + count, :] = value[
            row - start : row - start + count
        ].astype(BF16)
        row += count


def edge_kernel(
    rows, cols, fc_a, fc_b, x3, c3, w1_ref, gt, top3, low3, at_edge, slope, own, other, xe, ge, box
):
    even = is_even()
    for e in range(2):
        halo = [jnp.where(even, (fc_b, fc_a)[e][i], (fc_a, fc_b)[e][i]) for i in range(2)]
        acted = gelu_parts(halo[0].astype(F32))[2]
        shifts = column_shifts(acted)
        put_shifts(xe, e * cols, cols, shifts)
        at_edge[:, e * cols : (e + 1) * cols] = shifts[1].T
        put_shifts((top3, low3)[e], 0, cols, column_shifts(halo[1].astype(F32))[::-1])
    xtop, xlow = xe.at[0:cols], xe.at[cols : 2 * cols]
    for e, row in enumerate((0, rows - 1)):
        hidden = conv([window(x3, xtop, xlow, row - 1 + a, 1, rows, cols) for a in range(3)], w1_ref, NN)
        parts = gelu_parts(hidden)
        here = slice(e * cols, (e + 1) * cols)
        ge[:, here] = parts[2].astype(BF16).T
        slope[here, :] = gelu_slope(*parts)
    chans = w1_ref.shape[-1]
    for a in range(3):
        for b in range(3):
            part = slice(b * chans, (b + 1) * chans)
            total = dot(gt[...], c3[(2 - a) * cols : (rows - a) * cols, part])
            for e, row in enumerate((1 - a, rows - a)):
                ((ref, start, length),) = window(c3, top3, low3, row, 1, rows, cols)
                total += dot(ge[:, e * cols : (e + 1) * cols], ref[start : start + length, part])
            place(box, total, 3 * a + b)
    own[...] = box[0]
    other[...] = box[1]


def back_kernel(rows, cols, c3, top3, low3, w2_ref, slope, slope_edge, to_a, to_b, h3):
    block = rows // 2
    even = is_even()
    for first in (0, block):
        back = conv([window(c3, top3, low3, first + 1 - a, block, rows, cols) for a in range(3)], w2_ref, NT)
        for i in range(block):
            row = first + i
            if row == 0:
                factor = slope_edge[0:cols, :]
            elif row == rows - 1:
                factor = slope_edge[cols : 2 * cols, :]
            else:
                factor = slope[(row - 1) * cols : row * cols, :]
            value = (back[i * cols : (i + 1) * cols] * factor).astype(BF16)
            if row == 0:
                head = value
            if row == rows - 1:
                to_a[...] = jnp.where(even, value, head)
                to_b[...] = jnp.where(even, head, value)
            put_shifts(h3, row * cols, cols, column_shifts(value.astype(F32))[::-1])


def grad_kernel(rows, cols, at, at_edge, h3, own, other, box):
    chans = at.shape[0]
    for a in range(3):
        for b in range(3):
            part = slice(b * chans, (b + 1) * chans)
            if a == 1:
                total = dot(at[...], h3[:, part])
            elif a == 0:
                total = dot(at[:, : (rows - 1) * cols], h3[cols:, part])
                total += dot(at_edge[:, :cols], h3[:cols, part])
            else:
                total = dot(at[:, cols:], h3[: (rows - 1) * cols, part])
                total += dot(at_edge[:, cols:], h3[(rows - 1) * cols :, part])
            place(box, total, 3 * a + b)
    own[...] = box[0]
    other[...] = box[1]


def input_kernel(rows, cols, first, h3, got_a, got_b, f_ref, c_ref, w1_ref, *rest):
    out_ref, edge3 = rest[-2:]
    block = rows // 2
    even = is_even() if first == 0 else jnp.logical_not(is_even())
    halo = jnp.where(even, got_b[...], got_a[...])
    put_shifts(edge3, 0, cols, column_shifts(halo.astype(F32))[::-1])
    back = conv([window(h3, edge3, edge3, first + 1 - a, block, rows, cols) for a in range(3)], w1_ref, NT)
    here = slice(first * cols, (first + block) * cols)
    slope = gelu_slope(*gelu_parts(f_ref[here, :].astype(F32)))
    out_ref[...] = (c_ref[here, :].astype(F32) + back * slope).astype(BF16)


def pair_kernel(blocks, own, other, *outs):
    for k in range(blocks):
        outs[k][...] = (own[k].astype(F32) + other[k].astype(F32)).astype(BF16)


def chip_kernel(blocks, peers, *refs):
    terms, outs, whole, cut = refs[: 2 * blocks], refs[2 * blocks : 2 * blocks + peers], refs[-2], refs[-1]
    size = cut.shape[1]
    for g in range(2):
        total = terms[g * blocks][...].astype(F32)
        for k in range(1, blocks):
            total += terms[g * blocks + k][...].astype(F32)
        whole[...] = total
        for k in range(peers):
            cut[k] = whole[k * size : (k + 1) * size, :]
        for k in range(peers):
            outs[k][g] = cut[lax.axis_index("row") ^ k].astype(BF16)


def last_kernel(peers, scale, *refs):
    terms, outs = refs[:peers], refs[peers:]
    for g in range(2):
        total = terms[0][g].astype(F32)
        for k in range(1, peers):
            total += terms[k][g].astype(F32)
        total = total * scale
        size = total.shape[0]
        outs[g][pl.ds(0, size, stride=2), :] = total[:, :128]
        outs[g][pl.ds(1, size, stride=2), :] = total[:, 128:]


def call(kernel, outs, operands, scratch=(), flops=0, limit=24, specs=None, **extra):
    out_shape = tuple(jax.ShapeDtypeStruct(shape, dtype) for shape, dtype in outs)
    moved = sum(math.prod(shape) * jnp.dtype(dtype).itemsize for shape, dtype in outs)
    moved += sum(operand.size * operand.dtype.itemsize for operand in operands)
    return pl.pallas_call(
        kernel,
        out_shape=out_shape,
        in_specs=specs or [VMEM] * len(operands),
        out_specs=extra.pop("out_specs", tuple([VMEM] * len(outs))),
        scratch_shapes=list(scratch),
        cost_estimate=pl.CostEstimate(flops=flops, bytes_accessed=moved, transcendentals=0),
        compiler_params=pltpu.CompilerParams(vmem_limit_bytes=limit * MIB),
        **extra,
    )(*operands)


def flip(axis, bits):
    return [(i, i ^ bits) for i in range(lax.axis_size(axis))]


def neighbours(start, peers):
    pairs = [(i, i + 1) for i in range(start, peers - 1, 2)]
    return pairs + [(j, i) for i, j in pairs]


def local_part(features, cotangent, weight_one, weight_two):
    _, rows, cols, chans = features.shape
    peers = lax.axis_size("row")
    images = lax.axis_size("img")
    blocks = images // 2
    height = rows * peers
    cells = rows * cols
    size = 9 * chans // images
    cut = size // peers
    pairs_a, pairs_b = neighbours(0, peers), neighbours(1, peers)
    f_own = features.reshape(cells, chans)
    c_own = cotangent.reshape(cells, chans)
    ends = [pl.BlockSpec((cols, chans), lambda i, row=row: (row, 0)) for row in (0, rows - 1)]
    to_a, to_b = call(
        pack_kernel, [((2, cols, chans), BF16)] * 2, (f_own, f_own, c_own, c_own), specs=ends * 2, grid=(1,),
    )
    fc_a = lax.ppermute(to_a, "row", pairs_a)
    fc_b = lax.ppermute(to_b, "row", pairs_b)
    unit = 2 * cells * 9 * chans * chans
    wide = (cells, 3 * chans)
    pair = [((blocks, size, chans), BF16)] * 2
    box = pltpu.VMEM((2, blocks, size, chans), BF16)
    inner_cells = cells - 2 * cols
    sums = [((size, chans), BF16)] * blocks

    x3, c3, at, gt, slope = call(
        functools.partial(inner_kernel, rows, cols),
        [(wide, BF16), (wide, BF16), ((chans, cells), BF16), ((chans, inner_cells), BF16), ((inner_cells, chans), F32)],
        (f_own, c_own, weight_one), flops=unit,
    )
    top3, low3, at_edge, slope_edge, own_two, other_two = call(
        functools.partial(edge_kernel, rows, cols),
        [((cols, 3 * chans), BF16)] * 2 + [((chans, 2 * cols), BF16), ((2 * cols, chans), F32)] + pair,
        (fc_a, fc_b, x3, c3, weight_one, gt),
        scratch=[pltpu.VMEM((2 * cols, 3 * chans), BF16), pltpu.VMEM((chans, 2 * cols), BF16), box],
        flops=unit + unit // 4,
    )
    got_two = lax.ppermute(other_two, "img", flip("img", 1))
    to_a, to_b, h3 = call(
        functools.partial(back_kernel, rows, cols),
        [((cols, chans), BF16)] * 2 + [(wide, BF16)],
        (c3, top3, low3, weight_two, slope, slope_edge), flops=unit,
    )
    hg_a = lax.ppermute(to_a, "row", pairs_a)
    hg_b = lax.ppermute(to_b, "row", pairs_b)
    sums_two = call(functools.partial(pair_kernel, blocks), sums, (own_two, got_two))
    terms_two = [sums_two[0]]
    terms_two += [lax.ppermute(sums_two[k], "img", flip("img", 2 * k)) for k in range(1, blocks)]
    own_one, other_one = call(
        functools.partial(grad_kernel, rows, cols), pair, (at, at_edge, h3), scratch=[box], flops=unit,
    )
    got_one = lax.ppermute(other_one, "img", flip("img", 1))
    result = ()
    for part in range(2):
        result = call(
            functools.partial(input_kernel, rows, cols, part * (rows // 2)), [((cells, chans), BF16)],
            (h3, hg_a, hg_b, f_own, c_own, weight_one, *result), flops=unit // 2,
            scratch=[pltpu.VMEM((cols, 3 * chans), BF16)], grid=(1,),
            specs=[VMEM] * 6 + [pl.BlockSpec(memory_space=pl.ANY)] * part,
            out_specs=(pl.BlockSpec((cells // 2, chans), lambda i, part=part: (part, 0)),),
            input_output_aliases={6: 0} if part else {},
        )
    sums_one = call(functools.partial(pair_kernel, blocks), sums, (own_one, got_one))
    terms_one = [sums_one[0]]
    terms_one += [lax.ppermute(sums_one[k], "img", flip("img", 2 * k)) for k in range(1, blocks)]
    cuts = call(
        functools.partial(chip_kernel, blocks, peers), [((2, cut, chans), BF16)] * peers,
        (*terms_one, *terms_two),
        scratch=[pltpu.VMEM((size, chans), F32), pltpu.VMEM((peers, cut, chans), F32)],
    )
    terms = [cuts[0]] + [lax.ppermute(cuts[k], "row", flip("row", k)) for k in range(1, peers)]
    scale = 1.0 / math.sqrt(images * height * cols)
    one, two = call(functools.partial(last_kernel, peers, scale), [((2 * cut, 128), F32)] * 2, tuple(terms))
    return (result[0].reshape(features.shape), one.reshape(-1), two.reshape(-1))


def solution(mesh):
    placed = (P("img", "row", None, None), P("img", "row", None, None), P(), P())
    return jax.shard_map(
        local_part,
        mesh=mesh,
        in_specs=placed,
        out_specs=(P("img", "row", None, None), P(("img", "row")), P(("img", "row"))),
        check_vma=False,
    )
```

time: 124 us -> 64.2 us (0.52)
  waiting for transfers between devices: 44.5 us -> 6.98 us
  Pallas kernels: 39.1 us -> 29.7 us
  starting transfers between devices: 29.4 us -> 23.7 us
  local copies, waits for them, and re-layouts: 7.23 us -> 2.83 us
  other arithmetic: 2.24 us -> 0 us
    all_to_all x4 -> x0, waiting for transfers between devices: 30.2 us -> none  [exchange(): parts = lax.all_to_all(parts, axis, 0, 0)]
    all_to_all x4 -> x0, starting transfers between devices: 17.2 us -> none  [exchange(): parts = lax.all_to_all(parts, axis, 0, 0)]
    ppermute x4 -> x15, starting transfers between devices: 12.1 us -> 23.7 us  [the longest x3 5.48 us: local_part(): lax.ppermute(cuts[k], 'row', flip('row', k))]
    pallas_call x3 -> x11, Pallas kernels: 39.1 us -> 29.7 us  [call(): pl.pallas_call(kernel, out_shape=out_shape, in_specs=specs or [VMEM] * le...]
    ppermute x4 -> x15, waiting for transfers between devices: 14.3 us -> 6.98 us  [the longest x3 3.53 us: local_part(): lax.ppermute(sums_two[k], 'img', flip('img', 2 * k))]
    squeeze x1 -> x0, local copies, waits for them, and re-layouts: 2.12 us -> none  [shards(): wide[1]]
    reduce_sum x4 -> x0, other arithmetic: 1.71 us -> none  [exchange(): return jnp.sum(parts.astype(F32), axis=0)]
    unnamed x9 -> x12, local copies, waits for them, and re-layouts: 3.91 us -> 2.83 us
  transfers between devices with their start and end apart: 8 -> 15, of which waited for: 7 -> 5; matrix products, arithmetic and copies ran while one was open for 3% -> 0% of each run, Pallas kernels for 15% -> 23%
where the time goes in v1:
time: 64.2 us; the launch traced here: 64 us
  Pallas kernels  29.7 us (46%)
  starting transfers between devices  23.7 us (37%)
  waiting for transfers between devices  6.98 us (11%)
  local copies, waits for them, and re-layouts  2.83 us (4%)
  between operations  0.77 us (1%)
    pallas_call x11, Pallas kernels, call(): pl.pallas_call(kernel, out_shape=out_shape, in_specs=specs or [VMEM] * le...  29.7 us
    ppermute x3, starting transfers between devices, local_part(): lax.ppermute(cuts[k], 'row', flip('row', k))  5.48 us
    ppermute x3, starting transfers between devices, local_part(): lax.ppermute(sums_two[k], 'img', flip('img', 2 * k))  4.91 us
    ppermute x1, starting transfers between devices, local_part(): hg_a = lax.ppermute(to_a, 'row', pairs_a)  4.76 us
    ppermute x3, starting transfers between devices, local_part(): lax.ppermute(sums_one[k], 'img', flip('img', 2 * k))  3.55 us
    ppermute x3, waiting for transfers between devices, local_part(): lax.ppermute(sums_two[k], 'img', flip('img', 2 * k))  3.53 us
    ppermute x1, starting transfers between devices, local_part(): fc_a = lax.ppermute(to_a, 'row', pairs_a)  3.12 us
    unnamed x12, local copies, waits for them, and re-layouts  2.83 us
  transfers between devices with their start and end apart: 15, of which 5 were waited for; matrix products, arithmetic and copies ran while one was open for 0% of the time, Pallas kernels for 23%

profile of v1, /device:TPU:0, one launch (start us, length us, event | category | flops | bytes accessed | tf_op | source)
XLA Modules:
  0.0 64.0 jit_solution(16706565395344024789)
XLA Ops:
  0.6 1.4 %copy-done = bf16[1,8,384,256]{3,2,1,0:T(8,128)(2,1)S(1)} copy-done((bf16[1,8,384,256]{3,2,1,0:T(8,128)(2,1)S(1)}, bf16[1,8,384,256]{3,2,1,0:T(8,128)(2,1)}, u32[]{:S(2)}) %copy-start) | copy-done | bytes 1572888
  2.0 1.4 %copy-done.2 = bf16[1,8,384,256]{3,2,1,0:T(8,128)(2,1)S(1)} copy-done((bf16[1,8,384,256]{3,2,1,0:T(8,128)(2,1)S(1)}, bf16[1,8,384,256]{3,2,1,0:T(8,128)(2,1)}, u32[]{:S(2)}) %copy-start.2) | copy-done | bytes 1572888
  3.5 0.1 shard_map.68
  3.5 3.1 %collective-permute-start = (bf16[2,384,256]{2,1,0:T(8,128)(2,1)S(1)}, bf16[2,384,256]{2,1,0:T(8,128)(2,1)S(1)}, u32[]{:S(2)}, u32[]{:S(2)}) collective-permute-start(bf16[2,384,256]{2,1,0:T(8,128)(2,1)S(1)} %get-tuple-element.36), channel_id=1, source_target_pairs={{0,1},{2,3},{1,0},{3,2},{4,5},{6,7},{5,4},{7,6},{8,9},{10,11},{9,8... | collective-permute-start | bytes 1179656 | tf_op jit(solution)/shard_map/ppermute | solution.py:275
  6.7 0.7 %collective-permute-start.1 = (bf16[2,384,256]{2,1,0:T(8,128)(2,1)S(1)}, bf16[2,384,256]{2,1,0:T(8,128)(2,1)S(1)}, u32[]{:S(2)}, u32[]{:S(2)}) collective-permute-start(bf16[2,384,256]{2,1,0:T(8,128)(2,1)S(1)} %get-tuple-element.37), channel_id=1, source_target_pairs={{1,2},{2,1},{5,6},{6,5},{9,10},{10,9},{13,14},{14,13},{17,18},{18,... | collective-permute-start | bytes 1179656 | tf_op jit(solution)/shard_map/ppermute | solution.py:276
  7.3 7.1 %shard_map.67 = (bf16[3072,768]{1,0:T(8,128)(2,1)S(1)}, bf16[3072,768]{1,0:T(8,128)(2,1)S(1)}, bf16[256,3072]{1,0:T(8,128)(2,1)S(1)}, bf16[256,2304]{1,0:T(8,128)(2,1)S(1)}, f32[2304,256]{1,0:T(8,128)S(1)}) custom-call(bf16[3072,256]{1,0:T(8,128)(2,1)S(1)} %bitcast.7, bf16[3072,256]{1,0:T(8,128)(2,1)S(1)} %bitcast.12, bf16[3,3,256,256]{3,2,1,0:T(8,128)(2,1)S(1)} %copy-done.4), custom_call_target="tpu_custom_call" | custom-call | flops 3623878656 | bytes 18874368 | tf_op jit(solution)/shard_map/pallas_call | solution.py:238
  14.4 1.4 %collective-permute-done.fc_a = bf16[2,384,256]{2,1,0:T(8,128)(2,1)S(1)} collective-permute-done((bf16[2,384,256]{2,1,0:T(8,128)(2,1)S(1)}, bf16[2,384,256]{2,1,0:T(8,128)(2,1)S(1)}, u32[]{:S(2)}, u32[]{:S(2)}) %collective-permute-start) | collective-permute-done | bytes 393248 | tf_op jit(solution)/shard_map/ppermute | solution.py:275
  15.8 5.5 %shard_map.69 = (bf16[384,768]{1,0:T(8,128)(2,1)S(1)}, bf16[384,768]{1,0:T(8,128)(2,1)S(1)}, bf16[256,768]{1,0:T(8,128)(2,1)S(1)}, f32[768,256]{1,0:T(8,128)S(1)...) custom-call(bf16[2,384,256]{2,1,0:T(8,128)(2,1)S(1)} %collective-permute-done.fc_a, ...), custom_call_target="tpu_custom_call" | custom-call | flops 4529848320 | bytes 16121856 | tf_op jit(solution)/shard_map/pallas_call | solution.py:238
  21.3 4.5 %shard_map.70 = (bf16[384,256]{1,0:T(8,128)(2,1)S(1)}, bf16[384,256]{1,0:T(8,128)(2,1)S(1)}, bf16[3072,768]{1,0:T(8,128)(2,1)S(1)}) custom-call(bf16[3072,768]{1,0:T(8,128)(2,1)S(1)} %get-tuple-element.35.c3, bf16[384,768]{1,0:T(8,128)(2,1)S(1)} %get-tuple-element.40.top3, bf16[384,768]{1,0:T(8,128)(2,1)S(1)} %get-tuple-element.41.low3, ...), custom_call_target="tpu_custom_call" | custom-call | flops 3623878656 | bytes 15335424 | tf_op jit(solution)/shard_map/pallas_call | solution.py:238
  25.8 4.3 %shard_map.73 = (bf16[4,288,256]{2,1,0:T(8,128)(2,1)S(1)}, bf16[4,288,256]{2,1,0:T(8,128)(2,1)S(1)}) custom-call(bf16[256,3072]{1,0:T(8,128)(2,1)S(1)} %get-tuple-element.47.at, bf16[256,768]{1,0:T(8,128)(2,1)S(1)} %get-tuple-element.48.at_edge, bf16[3072,768]{1,0:T(8,128)(2,1)S(1)} %get-tuple-element.44.h3), custom_call_target="tpu_custom_call" | custom-call | flops 3623878656 | bytes 7864320 | tf_op jit(solution)/shard_map/pallas_call | solution.py:238
  30.2 0.5 collective-permute-start.8
  30.7 4.8 %collective-permute-start.2 = (bf16[384,256]{1,0:T(8,128)(2,1)S(1)}, bf16[384,256]{1,0:T(8,128)(2,1)S(1)}, u32[]{:S(2)}, u32[]{:S(2)}) collective-permute-start(bf16[384,256]{1,0:T(8,128)(2,1)S(1)} %get-tuple-element.45), channel_id=1, source_target_pairs={{0,1},{2,3},{1,0},{3,2},{4,5},{6,7},{5,4},{7,6},{8,9},{10,11},{9,8... | collective-permute-start | bytes 589832 | tf_op jit(solution)/shard_map/ppermute | solution.py:302
  35.5 0.7 %collective-permute-start.3 = (bf16[384,256]{1,0:T(8,128)(2,1)S(1)}, bf16[384,256]{1,0:T(8,128)(2,1)S(1)}, u32[]{:S(2)}, u32[]{:S(2)}) collective-permute-start(bf16[384,256]{1,0:T(8,128)(2,1)S(1)} %get-tuple-element.46), channel_id=1, source_target_pairs={{1,2},{2,1},{5,6},{6,5},{9,10},{10,9},{13,14},{14,13},{17,18},{18,... | collective-permute-start | bytes 589832 | tf_op jit(solution)/shard_map/ppermute | solution.py:303
  36.1 0.1 shard_map.74
  36.3 1.6 %collective-permute-start.5 = (bf16[288,256]{1,0:T(8,128)(2,1)S(1)}, bf16[288,256]{1,0:T(8,128)(2,1)S(1)}, u32[]{:S(2)}, u32[]{:S(2)}) collective-permute-start(bf16[288,256]{1,0:T(8,128)(2,1)S(1)} %get-tuple-element.52), channel_id=1, source_target_pairs={{0,8},{4,12},{8,0},{12,4},{16,24},{20,28},{24,16},{28,20},{1,9},{5... | collective-permute-start | bytes 442376 | tf_op jit(solution)/shard_map/ppermute | solution.py:323
  37.8 1.5 %collective-permute-start.6 = (bf16[288,256]{1,0:T(8,128)(2,1)S(1)}, bf16[288,256]{1,0:T(8,128)(2,1)S(1)}, u32[]{:S(2)}, u32[]{:S(2)}) collective-permute-start(bf16[288,256]{1,0:T(8,128)(2,1)S(1)} %get-tuple-element.53), channel_id=1, source_target_pairs={{0,16},{4,20},{8,24},{12,28},{16,0},{20,4},{24,8},{28,12},{1,17},{... | collective-permute-start | bytes 442376 | tf_op jit(solution)/shard_map/ppermute | solution.py:323
  39.4 0.5 collective-permute-start.7
  39.8 0.1 shard_map.75
  40.0 0.6 collective-permute-done.2.got_a
  40.6 1.5 %collective-permute-start.9 = (bf16[288,256]{1,0:T(8,128)(2,1)S(1)}, bf16[288,256]{1,0:T(8,128)(2,1)S(1)}, u32[]{:S(2)}, u32[]{:S(2)}) collective-permute-start(bf16[288,256]{1,0:T(8,128)(2,1)S(1)} %get-tuple-element.58), channel_id=1, source_target_pairs={{0,8},{4,12},{8,0},{12,4},{16,24},{20,28},{24,16},{28,20},{1,9},{5... | collective-permute-start | bytes 442376 | tf_op jit(solution)/shard_map/ppermute | solution.py:306
  42.1 1.5 %collective-permute-start.10 = (bf16[288,256]{1,0:T(8,128)(2,1)S(1)}, bf16[288,256]{1,0:T(8,128)(2,1)S(1)}, u32[]{:S(2)}, u32[]{:S(2)}) collective-permute-start(bf16[288,256]{1,0:T(8,128)(2,1)S(1)} %get-tuple-element.59), channel_id=1, source_target_pairs={{0,16},{4,20},{8,24},{12,28},{16,0},{20,4},{24,8},{28,12},{1,17},{... | collective-permute-start | bytes 442376 | tf_op jit(solution)/shard_map/ppermute | solution.py:306
  43.6 1.9 %collective-permute-start.11 = (bf16[288,256]{1,0:T(8,128)(2,1)S(1)}, bf16[288,256]{1,0:T(8,128)(2,1)S(1)}, u32[]{:S(2)}, u32[]{:S(2)}) collective-permute-start(bf16[288,256]{1,0:T(8,128)(2,1)S(1)} %get-tuple-element.60), channel_id=1, source_target_pairs={{0,24},{4,28},{8,16},{12,20},{16,8},{20,12},{24,0},{28,4},{1,25},{... | collective-permute-start | bytes 442376 | tf_op jit(solution)/shard_map/ppermute | solution.py:306
  45.5 3.5 %shard_map.71.rest_0_ = bf16[3072,256]{1,0:T(8,128)(2,1)} custom-call(bf16[3072,768]{1,0:T(8,128)(2,1)S(1)} %get-tuple-element.44.h3, bf16[384,256]{1,0:T(8,128)(2,1)S(1)} %collective-permute-done.2.got_a, bf16[384,256]{1,0:T(8,128)(2,1)S(1)} %collective-permute-done.3.got_b, bf16[3072,256]{1,0:T(8,128)(2,1)S(1)} %bitcast.8, bf16[3072,256]{1,0:T(8,128)(2,1)S(1)} %bitcast.13, ...), custom_call_target="tpu_custom_call" | custom-call | flops 1811939328 | bytes 11010048 | tf_op jit(solution)/shard_map/pallas_call | solution.py:238
  49.1 0.2 collective-permute-done.9.refs_5_
  49.2 3.4 %collective-permute-done.10.refs_6_ = bf16[288,256]{1,0:T(8,128)(2,1)S(1)} collective-permute-done((bf16[288,256]{1,0:T(8,128)(2,1)S(1)}, bf16[288,256]{1,0:T(8,128)(2,1)S(1)}, u32[]{:S(2)}, u32[]{:S(2)}) %collective-permute-start.10) | collective-permute-done | bytes 147488 | tf_op jit(solution)/shard_map/ppermute | solution.py:306
  52.6 0.2 shard_map.76
  52.8 3.0 %collective-permute-start.12 = (bf16[2,72,256]{2,1,0:T(8,128)(2,1)S(1)}, bf16[2,72,256]{2,1,0:T(8,128)(2,1)S(1)}, u32[]{:S(2)}, u32[]{:S(2)}) collective-permute-start(bf16[2,72,256]{2,1,0:T(8,128)(2,1)S(1)} %get-tuple-element.62), channel_id=1, source_target_pairs={{0,1},{1,0},{2,3},{3,2},{4,5},{5,4},{6,7},{7,6},{8,9},{9,8},{10,11... | collective-permute-start | bytes 221192 | tf_op jit(solution)/shard_map/ppermute | solution.py:329
  55.9 0.2 collective-permute-start.13
  56.1 2.2 %collective-permute-start.14 = (bf16[2,72,256]{2,1,0:T(8,128)(2,1)S(1)}, bf16[2,72,256]{2,1,0:T(8,128)(2,1)S(1)}, u32[]{:S(2)}, u32[]{:S(2)}) collective-permute-start(bf16[2,72,256]{2,1,0:T(8,128)(2,1)S(1)} %get-tuple-element.64), channel_id=1, source_target_pairs={{0,3},{1,2},{2,1},{3,0},{4,7},{5,6},{6,5},{7,4},{8,11},{9,10},{10,... | collective-permute-start | bytes 221192 | tf_op jit(solution)/shard_map/ppermute | solution.py:329
  58.3 3.6 %shard_map.72 = bf16[3072,256]{1,0:T(8,128)(2,1)} custom-call(bf16[3072,768]{1,0:T(8,128)(2,1)S(1)} %get-tuple-element.44.h3, bf16[384,256]{1,0:T(8,128)(2,1)S(1)} %collective-permute-done.2.got_a, bf16[384,256]{1,0:T(8,128)(2,1)S(1)} %collective-permute-done.3.got_b, bf16[3072,256]{1,0:T(8,128)(2,1)S(1)} %bitcast.9, ...), custom_call_target="tpu_custom_call", output_to_operand_aliasing={{}: (6, {})} | custom-call | flops 1811939328 | bytes 12582912 | tf_op jit(solution)/shard_map/pallas_call | solution.py:238
  61.9 1.5 %collective-permute-done.13.refs_2_ = bf16[2,72,256]{2,1,0:T(8,128)(2,1)S(1)} collective-permute-done((bf16[2,72,256]{2,1,0:T(8,128)(2,1)S(1)}, bf16[2,72,256]{2,1,0:T(8,128)(2,1)S(1)}, u32[]{:S(2)}, u32[]{:S(2)}) %collective-permute-start.13) | collective-permute-done | bytes 73760 | tf_op jit(solution)/shard_map/ppermute | solution.py:329
  63.4 0.7 %shard_map.77 = (f32[144,128]{1,0:T(8,128)}, f32[144,128]{1,0:T(8,128)}) custom-call(bf16[2,72,256]{2,1,0:T(8,128)(2,1)S(1)} %get-tuple-element.61.refs_0_, bf16[2,72,256]{2,1,0:T(8,128)(2,1)S(1)} %collective-permute-done.12.refs_1_, bf16[2,72,256]{2,1,0:T(8,128)(2,1)S(1)} %collective-permute-done.13.refs_2_, ...), custom_call_target="tpu_custom_call" | custom-call | bytes 442368 | tf_op jit(solution)/shard_map/pallas_call | solution.py:238
  (21 shorter events, 0.1 us)
Async XLA Ops:
  0.6 1.4 %copy-start = (bf16[1,8,384,256]{3,2,1,0:T(8,128)(2,1)S(1)}, bf16[1,8,384,256]{3,2,1,0:T(8,128)(2,1)}, u32[]{:S(2)}) copy-start(bf16[1,8,384,256]{3,2,1,0:T(8,128)(2,1)} %param.4) | copy-start | bytes 4718596
  2.0 1.4 %copy-start.2 = (bf16[1,8,384,256]{3,2,1,0:T(8,128)(2,1)S(1)}, bf16[1,8,384,256]{3,2,1,0:T(8,128)(2,1)}, u32[]{:S(2)}) copy-start(bf16[1,8,384,256]{3,2,1,0:T(8,128)(2,1)} %param.5) | copy-start | bytes 4718596
  3.4 3.9 %copy-start.4 = (bf16[3,3,256,256]{3,2,1,0:T(8,128)(2,1)S(1)}, bf16[3,3,256,256]{3,2,1,0:T(8,128)(2,1)}, u32[]{:S(2)}) copy-start(bf16[3,3,256,256]{3,2,1,0:T(8,128)(2,1)} %w1_ref.7) | copy-start | bytes 3538948
  3.5 12.2 %collective-permute-start = (bf16[2,384,256]{2,1,0:T(8,128)(2,1)S(1)}, bf16[2,384,256]{2,1,0:T(8,128)(2,1)S(1)}, u32[]{:S(2)}, u32[]{:S(2)}) collective-permute-start(bf16[2,384,256]{2,1,0:T(8,128)(2,1)S(1)} %get-tuple-element.36), channel_id=1, source_target_pairs={{0,1},{2,3},{1,0},{3,2},{4,5},{6,7},{5,4},{7,6},{8,9},{10,11},{9,8... | collective-permute-start | bytes 1179656 | tf_op jit(solution)/shard_map/ppermute | solution.py:275
  6.7 9.1 %collective-permute-start.1 = (bf16[2,384,256]{2,1,0:T(8,128)(2,1)S(1)}, bf16[2,384,256]{2,1,0:T(8,128)(2,1)S(1)}, u32[]{:S(2)}, u32[]{:S(2)}) collective-permute-start(bf16[2,384,256]{2,1,0:T(8,128)(2,1)S(1)} %get-tuple-element.37), channel_id=1, source_target_pairs={{1,2},{2,1},{5,6},{6,5},{9,10},{10,9},{13,14},{14,13},{17,18},{18,... | collective-permute-start | bytes 1179656 | tf_op jit(solution)/shard_map/ppermute | solution.py:276
  15.8 5.5 %copy-start.5 = (bf16[3,3,256,256]{3,2,1,0:T(8,128)(2,1)S(1)}, bf16[3,3,256,256]{3,2,1,0:T(8,128)(2,1)}, u32[]{:S(2)}) copy-start(bf16[3,3,256,256]{3,2,1,0:T(8,128)(2,1)} %w2_ref.1) | copy-start | bytes 3538948
  25.8 19.7 %copy-start.3 = (bf16[1,8,384,256]{3,2,1,0:T(8,128)(2,1)S(1)}, bf16[1,8,384,256]{3,2,1,0:T(8,128)(2,1)}, u32[]{:S(2)}) copy-start(bf16[1,8,384,256]{3,2,1,0:T(8,128)(2,1)} %param.5) | copy-start | bytes 4718596
  30.1 15.4 %copy-start.1 = (bf16[1,8,384,256]{3,2,1,0:T(8,128)(2,1)S(1)}, bf16[1,8,384,256]{3,2,1,0:T(8,128)(2,1)}, u32[]{:S(2)}) copy-start(bf16[1,8,384,256]{3,2,1,0:T(8,128)(2,1)} %param.4) | copy-start | bytes 4718596
  30.1 6.0 %collective-permute-start.4 = (bf16[4,288,256]{2,1,0:T(8,128)(2,1)S(1)}, bf16[4,288,256]{2,1,0:T(8,128)(2,1)S(1)}, u32[]{:S(2)}, u32[]{:S(2)}) collective-permute-start(bf16[4,288,256]{2,1,0:T(8,128)(2,1)S(1)} %get-tuple-element.50), channel_id=1, source_target_pairs={{0,4},{4,0},{8,12},{12,8},{16,20},{20,16},{24,28},{28,24},{1,5},{5... | collective-permute-start | bytes 1769480 | tf_op jit(solution)/shard_map/ppermute | solution.py:310
  30.2 9.2 %collective-permute-start.8 = (bf16[4,288,256]{2,1,0:T(8,128)(2,1)S(1)}, bf16[4,288,256]{2,1,0:T(8,128)(2,1)S(1)}, u32[]{:S(2)}, u32[]{:S(2)}) collective-permute-start(bf16[4,288,256]{2,1,0:T(8,128)(2,1)S(1)} %get-tuple-element.56), channel_id=1, source_target_pairs={{0,4},{4,0},{8,12},{12,8},{16,20},{20,16},{24,28},{28,24},{1,5},{5... | collective-permute-start | bytes 1769480 | tf_op jit(solution)/shard_map/ppermute | solution.py:296
  30.7 9.9 %collective-permute-start.2 = (bf16[384,256]{1,0:T(8,128)(2,1)S(1)}, bf16[384,256]{1,0:T(8,128)(2,1)S(1)}, u32[]{:S(2)}, u32[]{:S(2)}) collective-permute-start(bf16[384,256]{1,0:T(8,128)(2,1)S(1)} %get-tuple-element.45), channel_id=1, source_target_pairs={{0,1},{2,3},{1,0},{3,2},{4,5},{6,7},{5,4},{7,6},{8,9},{10,11},{9,8... | collective-permute-start | bytes 589832 | tf_op jit(solution)/shard_map/ppermute | solution.py:302
  35.5 6.6 %collective-permute-start.3 = (bf16[384,256]{1,0:T(8,128)(2,1)S(1)}, bf16[384,256]{1,0:T(8,128)(2,1)S(1)}, u32[]{:S(2)}, u32[]{:S(2)}) collective-permute-start(bf16[384,256]{1,0:T(8,128)(2,1)S(1)} %get-tuple-element.46), channel_id=1, source_target_pairs={{1,2},{2,1},{5,6},{6,5},{9,10},{10,9},{13,14},{14,13},{17,18},{18,... | collective-permute-start | bytes 589832 | tf_op jit(solution)/shard_map/ppermute | solution.py:303
  36.3 7.3 %collective-permute-start.5 = (bf16[288,256]{1,0:T(8,128)(2,1)S(1)}, bf16[288,256]{1,0:T(8,128)(2,1)S(1)}, u32[]{:S(2)}, u32[]{:S(2)}) collective-permute-start(bf16[288,256]{1,0:T(8,128)(2,1)S(1)} %get-tuple-element.52), channel_id=1, source_target_pairs={{0,8},{4,12},{8,0},{12,4},{16,24},{20,28},{24,16},{28,20},{1,9},{5... | collective-permute-start | bytes 442376 | tf_op jit(solution)/shard_map/ppermute | solution.py:323
  37.8 11.2 %collective-permute-start.6 = (bf16[288,256]{1,0:T(8,128)(2,1)S(1)}, bf16[288,256]{1,0:T(8,128)(2,1)S(1)}, u32[]{:S(2)}, u32[]{:S(2)}) collective-permute-start(bf16[288,256]{1,0:T(8,128)(2,1)S(1)} %get-tuple-element.53), channel_id=1, source_target_pairs={{0,16},{4,20},{8,24},{12,28},{16,0},{20,4},{24,8},{28,12},{1,17},{... | collective-permute-start | bytes 442376 | tf_op jit(solution)/shard_map/ppermute | solution.py:323
  39.4 9.7 %collective-permute-start.7 = (bf16[288,256]{1,0:T(8,128)(2,1)S(1)}, bf16[288,256]{1,0:T(8,128)(2,1)S(1)}, u32[]{:S(2)}, u32[]{:S(2)}) collective-permute-start(bf16[288,256]{1,0:T(8,128)(2,1)S(1)} %get-tuple-element.54), channel_id=1, source_target_pairs={{0,24},{4,28},{8,16},{12,20},{16,8},{20,12},{24,0},{28,4},{1,25},{... | collective-permute-start | bytes 442376 | tf_op jit(solution)/shard_map/ppermute | solution.py:323
  40.6 8.6 %collective-permute-start.9 = (bf16[288,256]{1,0:T(8,128)(2,1)S(1)}, bf16[288,256]{1,0:T(8,128)(2,1)S(1)}, u32[]{:S(2)}, u32[]{:S(2)}) collective-permute-start(bf16[288,256]{1,0:T(8,128)(2,1)S(1)} %get-tuple-element.58), channel_id=1, source_target_pairs={{0,8},{4,12},{8,0},{12,4},{16,24},{20,28},{24,16},{28,20},{1,9},{5... | collective-permute-start | bytes 442376 | tf_op jit(solution)/shard_map/ppermute | solution.py:306
  42.1 10.5 %collective-permute-start.10 = (bf16[288,256]{1,0:T(8,128)(2,1)S(1)}, bf16[288,256]{1,0:T(8,128)(2,1)S(1)}, u32[]{:S(2)}, u32[]{:S(2)}) collective-permute-start(bf16[288,256]{1,0:T(8,128)(2,1)S(1)} %get-tuple-element.59), channel_id=1, source_target_pairs={{0,16},{4,20},{8,24},{12,28},{16,0},{20,4},{24,8},{28,12},{1,17},{... | collective-permute-start | bytes 442376 | tf_op jit(solution)/shard_map/ppermute | solution.py:306
  43.6 9.0 %collective-permute-start.11 = (bf16[288,256]{1,0:T(8,128)(2,1)S(1)}, bf16[288,256]{1,0:T(8,128)(2,1)S(1)}, u32[]{:S(2)}, u32[]{:S(2)}) collective-permute-start(bf16[288,256]{1,0:T(8,128)(2,1)S(1)} %get-tuple-element.60), channel_id=1, source_target_pairs={{0,24},{4,28},{8,16},{12,20},{16,8},{20,12},{24,0},{28,4},{1,25},{... | collective-permute-start | bytes 442376 | tf_op jit(solution)/shard_map/ppermute | solution.py:306
  52.8 9.1 %collective-permute-start.12 = (bf16[2,72,256]{2,1,0:T(8,128)(2,1)S(1)}, bf16[2,72,256]{2,1,0:T(8,128)(2,1)S(1)}, u32[]{:S(2)}, u32[]{:S(2)}) collective-permute-start(bf16[2,72,256]{2,1,0:T(8,128)(2,1)S(1)} %get-tuple-element.62), channel_id=1, source_target_pairs={{0,1},{1,0},{2,3},{3,2},{4,5},{5,4},{6,7},{7,6},{8,9},{9,8},{10,11... | collective-permute-start | bytes 221192 | tf_op jit(solution)/shard_map/ppermute | solution.py:329
  55.9 7.5 %collective-permute-start.13 = (bf16[2,72,256]{2,1,0:T(8,128)(2,1)S(1)}, bf16[2,72,256]{2,1,0:T(8,128)(2,1)S(1)}, u32[]{:S(2)}, u32[]{:S(2)}) collective-permute-start(bf16[2,72,256]{2,1,0:T(8,128)(2,1)S(1)} %get-tuple-element.63), channel_id=1, source_target_pairs={{0,2},{1,3},{2,0},{3,1},{4,6},{5,7},{6,4},{7,5},{8,10},{9,11},{10,... | collective-permute-start | bytes 221192 | tf_op jit(solution)/shard_map/ppermute | solution.py:329
  56.1 7.3 %collective-permute-start.14 = (bf16[2,72,256]{2,1,0:T(8,128)(2,1)S(1)}, bf16[2,72,256]{2,1,0:T(8,128)(2,1)S(1)}, u32[]{:S(2)}, u32[]{:S(2)}) collective-permute-start(bf16[2,72,256]{2,1,0:T(8,128)(2,1)S(1)} %get-tuple-element.64), channel_id=1, source_target_pairs={{0,3},{1,2},{2,1},{3,0},{4,7},{5,6},{6,5},{7,4},{8,11},{9,10},{10,... | collective-permute-start | bytes 221192 | tf_op jit(solution)/shard_map/ppermute | solution.py:329
